TPU v7x, 32 devices: a whole 2x2x4 slice. The times are simulated.
32 devices in a mesh: batch: 16 (over z, y, x), strip: 2 (over core).
Axes of the slice: x: 2, y: 2, z: 4, core: 2. Of those that a mesh axis runs over, the one named last changes fastest.
Arguments:
- state_maps: bfloat16 [16, 32, 64, 256], P('batch', 'strip'), may hold values from -6 to 6
- goal_maps: bfloat16 [16, 32, 64, 256], P('batch', 'strip'), may hold values from -6 to 6
- conv_one: bfloat16 [3, 3, 256, 256], replicated, may hold values from -0.125 to 0.125
- conv_two: bfloat16 [3, 3, 256, 256], replicated, may hold values from -0.125 to 0.125
- state_proj: bfloat16 [256, 1024], replicated, may hold values from -0.375 to 0.375
- goal_proj: bfloat16 [256, 1024], replicated, may hold values from -0.375 to 0.375
- inv_temp: float32 [1], replicated, may hold values from 4 to 16
- pair_index: int32 [16], P('batch'), may hold values from 0 to 15, each once
Outputs:
- pair_loss: float32 [16], P('batch')
- grad_state_proj: float32 [256, 1024], replicated
- grad_goal_proj: float32 [256, 1024], replicated
- block_maps: float32 [2, 16, 32, 64, 256], P(None, 'batch', 'strip')
Inputs may be any that keep to these rules, and one draw needn't show every extreme that they name: pair_index names each goal of 0 to 15 exactly once.
All inputs are finite; a program needn't handle non-finite values.
Results may differ from a plain program's by a relative error of at most 0.017.
Values may be sent and summed in bfloat16 or wider, within the bound.
A program may use at most 64 MiB of HBM per device.

v0:
```python
import jax
import jax.numpy as jnp
from jax import lax
from jax.sharding import PartitionSpec as P


def extended(cells, sides, width):
    for axis, dim in sides:
        count = lax.axis_size(axis)
        ends = count - 1
        head = lax.slice_in_dim(cells, 0, width, axis=dim)
        tail = lax.slice_in_dim(cells, cells.shape[dim] - width, cells.shape[dim], axis=dim)
        cells = jnp.concatenate(
            [
                lax.ppermute(tail, axis, [(i, (i + 1) % count) for i in range(ends)]),
                cells,
                lax.ppermute(head, axis, [((i + 1) % count, i) for i in range(ends)]),
            ],
            axis=dim,
        )
    return cells


def conv_rows(padded, kernel):
    return lax.conv_general_dilated(
        padded,
        kernel,
        (1, 1),
        ((0, 0), (1, 1)),
        dimension_numbers=("NHWC", "HWIO", "NHWC"),
        preferred_element_type=jnp.float32,
    )


def normalize(embedding):
    inverse_norm = lax.rsqrt(jnp.sum(embedding * embedding, axis=-1, keepdims=True) + 1e-06)
    return (embedding * inverse_norm, inverse_norm)


def shards(state_maps, goal_maps, conv_one, conv_two, state_proj, goal_proj, inv_temp, pair_index):
    local_pairs = state_maps.shape[0]
    strip_rows = state_maps.shape[1]
    columns = state_maps.shape[2]
    channels = state_maps.shape[3]
    frames = jnp.concatenate([state_maps, goal_maps], axis=0)
    active = jnp.maximum(frames, 0)
    padded = extended(active, (("strip", 1),), 1)
    first_out = jnp.maximum(conv_rows(padded, conv_one), 0.0).astype(jnp.bfloat16)
    padded_two = extended(first_out, (("strip", 1),), 1)
    block_out = jnp.maximum(frames.astype(jnp.float32) + conv_rows(padded_two, conv_two), 0.0)
    block_maps = block_out.reshape((2, local_pairs, strip_rows, columns, channels))
    total_cells = strip_rows * lax.axis_size("strip") * columns
    partial_value = jnp.sum(block_out, axis=(1, 2)) / total_cells
    pooled = lax.psum(partial_value, "strip")
    pooled_bf = pooled.astype(jnp.bfloat16)
    state_pool = pooled_bf[0:1]
    goal_pool = pooled_bf[1:2]
    state_emb = jnp.dot(state_pool, state_proj, preferred_element_type=jnp.float32)
    goal_emb = jnp.dot(goal_pool, goal_proj, preferred_element_type=jnp.float32)
    state_unit, state_inverse = normalize(state_emb)
    goal_unit, goal_inverse = normalize(goal_emb)
    state_bf = state_unit.astype(jnp.bfloat16)
    goal_bf = goal_unit.astype(jnp.bfloat16)
    goals_all = lax.all_gather(goal_bf, "batch", axis=0, tiled=True)
    sharpness = inv_temp[0]
    logits = sharpness * jnp.einsum(
        "ie,je->ij", state_bf, goals_all, preferred_element_type=jnp.float32
    )
    exp_logits = jnp.exp(logits)
    row_total = jnp.sum(exp_logits, axis=1)
    matched = jnp.arange(goals_all.shape[0], dtype=jnp.int32)[None, :] == pair_index[:, None]
    positive = jnp.sum(jnp.where(matched, logits, 0.0), axis=1)
    pair_loss = jnp.log(row_total) - positive
    logit_grad = (exp_logits / row_total[:, None] - matched.astype(jnp.float32)).astype(
        jnp.bfloat16
    )
    state_unit_grad = sharpness * jnp.dot(logit_grad, goals_all, preferred_element_type=jnp.float32)
    picked = lax.slice_in_dim(logit_grad, 0, 1 * lax.axis_size("batch"), axis=1)
    goal_unit_grad = lax.psum_scatter(
        sharpness * jnp.einsum("ij,ie->je", picked, state_bf, preferred_element_type=jnp.float32),
        "batch",
        scatter_dimension=0,
        tiled=True,
    )
    state_emb_grad = (
        state_unit_grad - state_unit * jnp.sum(state_unit * state_unit_grad, axis=-1, keepdims=True)
    ) * state_inverse
    goal_emb_grad = (
        goal_unit_grad - goal_unit * jnp.sum(goal_unit * goal_unit_grad, axis=-1, keepdims=True)
    ) * goal_inverse
    emb_grad_bf = jnp.stack([state_emb_grad, goal_emb_grad], axis=0).astype(jnp.bfloat16)
    pool_pair = jnp.stack([state_pool, goal_pool], axis=0)
    empty = jnp.zeros((channels, state_proj.shape[1]), jnp.float32)
    pool_piece = lax.all_gather(pool_pair, "batch", axis=1, tiled=True)
    grad_piece = lax.all_gather(emb_grad_bf, "batch", axis=1, tiled=True)
    state_sum = empty + jnp.einsum(
        "ic,ie->ce", pool_piece[0], grad_piece[0], preferred_element_type=jnp.float32
    )
    goal_sum = empty + jnp.einsum(
        "ic,ie->ce", pool_piece[1], grad_piece[1], preferred_element_type=jnp.float32
    )
    return (pair_loss, state_sum, goal_sum, block_maps)


def solution(mesh):
    placed = (
        P("batch", "strip", None, None),
        P("batch", "strip", None, None),
        P(),
        P(),
        P(),
        P(),
        P(),
        P("batch"),
    )
    return jax.shard_map(
        shards,
        mesh=mesh,
        in_specs=placed,
        out_specs=(P("batch"), P(), P(), P(None, "batch", "strip", None, None)),
        check_vma=False,
    )
```

profile of v0, /device:TPU:0, one launch (start us, length us, event | category | flops | bytes accessed | tf_op | source)
XLA Modules:
  0.0 284.3 jit_solution(8985306626940305975)
XLA Ops:
  7.2 1.4 copy_dynamic-update-slice_fusion.1
  8.7 1.3 copy_dynamic-update-slice_fusion
  11.3 2.4 collective-permute-start
  13.7 1.3 collective-permute-start.1
  20.4 1.5 fusion.4
  21.9 2.9 %maximum_convert_fusion = bf16[16,16,9,256]{3,1,2,0:T(8,128)(2,1)S(1)} fusion(bf16[3,3,256,256]{3,2,1,0:T(8,128)(2,1)S(1)} %copy-done, bf16[18,2,8,11,256]{4,1,3,2,0:T(2,128)(2,1)S(1)} %fusion.4, pred[16,9]{0,1:T(8,128)(4,1)S(1)} %copy-done.5), kind=kOutput, calls=%fused_computation.3 | convolution fusion | flops 2719678464 | bytes 3981456 | tf_op jit(solution)/shard_map/conv_general_dilated | solution.py:25
  25.4 3.0 %collective-permute-start.2 = (bf16[2,1,64,256]{3,2,0,1:T(8,128)(2,1)S(1)}, bf16[2,1,64,256]{3,2,0,1:T(8,128)(2,1)S(1)}, u32[]{:S(2)}, u32[]{:S(2)}) collective-permute-start(bf16[2,1,64,256]{3,2,0,1:T(8,128)(2,1)S(1)} %slice_bitcast_fusion.3), channel_id=1, source_target_pairs={{0,1},{2,3},{4,5},{6,7},{8,9},{10,11},{12,13},{14,15},{16,17},{18,... | collective-permute-start | bytes 196616 | tf_op jit(solution)/shard_map/ppermute | solution.py:15
  28.7 1.5 collective-permute-start.3
  30.3 1.6 collective-permute-done.3
  35.4 1.5 fusion.5
  36.9 3.1 %fusion.12 = f32[16,16,9,256]{3,1,2,0:T(8,128)S(1)} fusion(bf16[3,3,256,256]{3,2,1,0:T(8,128)(2,1)S(1)} %copy-done.3, bf16[18,2,8,11,256]{4,1,3,2,0:T(2,128)(2,1)S(1)} %fusion.5, pred[16,9]{0,1:T(8,128)(4,1)S(1)} %copy-done.5), kind=kOutput, calls=%fused_computation.17 | convolution fusion | flops 2718498816 | bytes 5161104 | tf_op jit(solution)/shard_map/conv_general_dilated | solution.py:25
  40.0 1.4 copy.63
  41.8 2.5 psum.7
  44.3 1.2 fusion.22
  46.8 1.2 fusion.24
  49.4 41.8 %all_gather.10 = bf16[2,16,256]{2,0,1:T(2,128)(2,1)S(1)} all-gather(bf16[2,1,256]{2,0,1:T(2,128)(2,1)S(1)} %pad_maximum_fusion.1), channel_id=1, replica_groups=mesh['batch'=16,'strip'=2] {'batch'}, dimensions={1}, use_global_device_ids=true | all-gather | bytes 17408 | tf_op jit(solution)/shard_map/all_gather | solution.py:94
  91.2 35.6 %all-gather = bf16[16384]{0:T(1024)(128)(2,1)S(1)} all-gather(bf16[1024]{0:T(1024)(128)(2,1)S(1)} %get-tuple-element.26), channel_id=2, replica_groups=mesh['batch'=16,'strip'=2] {'batch'}, dimensions={0}, use_global_device_ids=true | all-gather | bytes 34816 | tf_op jit(solution)/shard_map/all_gather | solution.py:64
  131.1 2.5 copy.68
  134.3 96.3 %all-reduce.3.cloned.1.call-done = f32[16,1024]{1,0:T(8,128)} async-done(((f32[16,1024]{1,0:T(8,128)}), f32[16,1024]{1,0:T(8,128)}) %all-reduce.3.cloned.1.call-update) | async-done | bytes 65552
  230.5 2.0 multiply_reduce_fusion
  233.2 1.4 convert_bitcast_fusion
  234.6 39.1 %all_gather.11 = bf16[2,16,1024]{2,0,1:T(2,128)(2,1)S(1)} all-gather(bf16[2,1,1024]{2,0,1:T(2,128)(2,1)S(1)} %pad_maximum_fusion), channel_id=1, replica_groups=mesh['batch'=16,'strip'=2] {'batch'}, dimensions={1}, use_global_device_ids=true | all-gather | bytes 69632 | tf_op jit(solution)/shard_map/all_gather | solution.py:95
  273.7 1.3 fusion.20
  275.0 1.3 fusion.21
  (60 shorter events, 15.6 us)
Async XLA Ops:
  7.2 14.8 %copy-start = (bf16[3,3,256,256]{3,2,1,0:T(8,128)(2,1)S(1)}, bf16[3,3,256,256]{3,2,1,0:T(8,128)(2,1)}, u32[]{:S(2)}) copy-start(bf16[3,3,256,256]{3,2,1,0:T(8,128)(2,1)} %param.10) | copy-start | bytes 3538948
  7.2 223.3 %all-reduce.3.cloned.1.call-start = ((), (), s32[]{:S(2)}) async-start(), calls=%async_computation | async-start | bytes 131072
  8.6 7.6 %copy-start.4 = (u32[32]{0:T(128)S(1)}, u32[32]{0:T(128)}, u32[]{:S(2)}) copy-start(u32[32]{0:T(128)} %constant.27) | copy-start | bytes 388
  10.0 1.0 copy-start.1
  11.3 5.6 %collective-permute-start = (bf16[2,1,64,256]{3,1,2,0:T(2,128)(2,1)S(1)}, bf16[2,1,64,256]{3,1,2,0:T(2,128)(2,1)S(1)}, u32[]{:S(2)}, u32[]{:S(2)}) collective-permute-start(bf16[2,1,64,256]{3,1,2,0:T(2,128)(2,1)S(1)} %get-tuple-element.32), channel_id=1, source_target_pairs={{0,1},{2,3},{4,5},{6,7},{8,9},{10,11},{12,13},{14,15},{16,17},{18,... | collective-permute-start | bytes 196616 | tf_op jit(solution)/shard_map/ppermute | solution.py:15
  13.7 3.2 %collective-permute-start.1 = (bf16[2,1,64,256]{3,1,2,0:T(2,128)(2,1)S(1)}, bf16[2,1,64,256]{3,1,2,0:T(2,128)(2,1)S(1)}, u32[]{:S(2)}, u32[]{:S(2)}) collective-permute-start(bf16[2,1,64,256]{3,1,2,0:T(2,128)(2,1)S(1)} %get-tuple-element.33), channel_id=1, source_target_pairs={{1,0},{3,2},{5,4},{7,6},{9,8},{11,10},{13,12},{15,14},{17,16},{19,... | collective-permute-start | bytes 196616 | tf_op jit(solution)/shard_map/ppermute | solution.py:17
  20.4 1.5 copy-start.5
  25.4 4.8 %collective-permute-start.2 = (bf16[2,1,64,256]{3,2,0,1:T(8,128)(2,1)S(1)}, bf16[2,1,64,256]{3,2,0,1:T(8,128)(2,1)S(1)}, u32[]{:S(2)}, u32[]{:S(2)}) collective-permute-start(bf16[2,1,64,256]{3,2,0,1:T(8,128)(2,1)S(1)} %slice_bitcast_fusion.3), channel_id=1, source_target_pairs={{0,1},{2,3},{4,5},{6,7},{8,9},{10,11},{12,13},{14,15},{16,17},{18,... | collective-permute-start | bytes 196616 | tf_op jit(solution)/shard_map/ppermute | solution.py:15
  28.7 3.2 %collective-permute-start.3 = (bf16[2,1,64,256]{3,1,2,0:T(2,128)(2,1)S(1)}, bf16[2,1,64,256]{3,1,2,0:T(2,128)(2,1)S(1)}, u32[]{:S(2)}, u32[]{:S(2)}) collective-permute-start(bf16[2,1,64,256]{3,1,2,0:T(2,128)(2,1)S(1)} %copy.59), channel_id=1, source_target_pairs={{1,0},{3,2},{5,4},{7,6},{9,8},{11,10},{13,12},{15,14},{17,16},{19,... | collective-permute-start | bytes 196616 | tf_op jit(solution)/shard_map/ppermute | solution.py:17
  35.4 1.5 copy-start.3
  40.0 1.4 copy-start.2
Sparse Core Ops, SparseCore 0:
  129.3 101.2 all-reduce.2
where the time goes:
time: 285 us; the launch traced here: 284 us
  blocking collectives  119 us (42%)
  waiting for transfers between devices  97.9 us (34%)
  between operations  19.6 us (7%)
  local copies, waits for them, and re-layouts  14.3 us (5%)
  other arithmetic  13.4 us (5%)
  matrix products  11.9 us (4%)
  starting transfers between devices  8.23 us (3%)
    unnamed x2, waiting for transfers between devices  96.3 us
    all_gather x1, blocking collectives, shards(): pool_piece = lax.all_gather(pool_pair, 'batch', axis=1, tiled=True)  41.8 us
    all_gather x1, blocking collectives, shards(): grad_piece = lax.all_gather(emb_grad_bf, 'batch', axis=1, tiled=True)  39.1 us
    all_gather x1, blocking collectives, shards(): goals_all = lax.all_gather(goal_bf, 'batch', axis=0, tiled=True)  35.6 us
    unnamed x17, local copies, waits for them, and re-layouts  8 us
    conv_general_dilated x2, matrix products, conv_rows(): lax.conv_general_dilated(padded, kernel, (1, 1), ((0, 0), (1, 1)), dimens...  6.02 us
  transfers between devices with their start and end apart: 5, of which 2 were waited for; matrix products, arithmetic and copies ran while one was open for 2% of the time, Pallas kernels for 0%

commit v1 on v0

v1 whole, which is shorter than its diff:
```python
import functools

import jax
import jax.numpy as jnp
from jax import lax
from jax.experimental import pallas as pl
from jax.experimental.pallas import tpu as pltpu
from jax.sharding import PartitionSpec as P

MESH = pl.DeviceIdType.MESH
BF = jnp.bfloat16
F32 = jnp.float32
LANES = 128


def spread(dst, frame, row, cells):
    rows, columns, channels = cells.shape
    where = lax.broadcasted_iota(jnp.int32, cells.shape, 1)
    left = jnp.where(where == 0, 0.0, pltpu.roll(cells, 1, axis=1))
    right = jnp.where(where == columns - 1, 0.0, pltpu.roll(cells, columns - 1, axis=1))
    span = pl.ds(row, rows)
    dst[frame, span, :, 0:channels] = left.astype(BF)
    dst[frame, span, :, channels : 2 * channels] = cells.astype(BF)
    dst[frame, span, :, 2 * channels : 3 * channels] = right.astype(BF)


def taps(src, frame, row, rows):
    columns, width = src.shape[2], src.shape[3]
    return jnp.concatenate(
        [src[frame, row + d : row + d + rows].reshape(rows * columns, width) for d in range(3)],
        axis=1,
    )


def block_kernel(
    batches, strips,
    state_ref, goal_ref, one_ref, two_ref, sproj_ref, gproj_ref, index_ref,
    block_ref, gathered_ref, sproj_out, gproj_out,
    maps, wide_one, wide_two, w_one, w_two, halo, part, parts, note, notes,
    load_sem, halo_send, halo_recv, part_send, part_recv, note_send, note_recv,
):
    b = lax.axis_index("batch")
    s = lax.axis_index("strip")
    rows, columns, channels = maps.shape[1], maps.shape[2], maps.shape[3]
    packs = channels // LANES

    loads = [
        pltpu.make_async_copy(state_ref.at[0], maps.at[0], load_sem.at[0]),
        pltpu.make_async_copy(one_ref, w_one, load_sem.at[1]),
        pltpu.make_async_copy(goal_ref.at[0], maps.at[1], load_sem.at[2]),
        pltpu.make_async_copy(two_ref, w_two, load_sem.at[3]),
        pltpu.make_async_copy(sproj_ref, sproj_out, load_sem.at[4]),
        pltpu.make_async_copy(gproj_ref, gproj_out, load_sem.at[5]),
    ]
    for copy in loads:
        copy.start()

    @pl.when(s == 0)
    def _():
        halo[0] = jnp.zeros(halo.shape[1:], BF)

    @pl.when(s == strips - 1)
    def _():
        halo[1] = jnp.zeros(halo.shape[1:], BF)

    barrier = pltpu.get_barrier_semaphore()

    def greet_strip(k, carry):
        pl.semaphore_signal(barrier, inc=1, device_id=(b, lax.rem(s + k, strips)), device_id_type=MESH)
        return carry

    def greet_batch(k, carry):
        pl.semaphore_signal(barrier, inc=1, device_id=(lax.rem(b + k, batches), s), device_id_type=MESH)
        return carry

    lax.fori_loop(1, batches, greet_batch, 0)
    lax.fori_loop(1, strips, greet_strip, 0)

    def first(lhs):
        return jnp.maximum(jnp.dot(lhs, w_one[...], preferred_element_type=F32), 0.0)

    def second(lhs, skip):
        return jnp.maximum(skip + jnp.dot(lhs, w_two[...], preferred_element_type=F32), 0.0)

    half = (rows - 2) // 2
    for f in range(2):
        loads[2 * f].wait()
        spread(wide_one, f, 2, jnp.maximum(maps[f].astype(F32), 0.0))
        if f == 0:
            loads[1].wait()
        for r in range(1, rows - 1, half):
            out = first(taps(wide_one, f, r + 1, half))
            spread(wide_two, f, r + 1, out.reshape(half, columns, channels))

    pl.semaphore_wait(barrier, strips + batches - 2)
    down = pltpu.make_async_remote_copy(
        src_ref=maps.at[:, rows - 2 : rows], dst_ref=halo.at[0],
        send_sem=halo_send.at[0], recv_sem=halo_recv.at[0],
        device_id=(b, lax.rem(s + 1, strips)), device_id_type=MESH,
    )
    up = pltpu.make_async_remote_copy(
        src_ref=maps.at[:, 0:2], dst_ref=halo.at[1],
        send_sem=halo_send.at[1], recv_sem=halo_recv.at[1],
        device_id=(b, lax.rem(s + strips - 1, strips)), device_id_type=MESH,
    )

    @pl.when(s < strips - 1)
    def _():
        down.start()

    @pl.when(s > 0)
    def _():
        up.start()

    loads[3].wait()
    sums = []
    half = (rows - 4) // 2
    for f in range(2):
        total = jnp.zeros((1, channels), F32)
        for r in range(2, rows - 2, half):
            skip = maps[f, r : r + half].reshape(half * columns, channels).astype(F32)
            out = second(taps(wide_two, f, r, half), skip)
            block_ref[f, 0, r : r + half] = out.reshape(half, columns, channels)
            total = total + jnp.sum(out, axis=0, keepdims=True)
        sums.append(total)

    @pl.when(s < strips - 1)
    def _():
        down.wait_send()
        up.wait_recv()

    @pl.when(s > 0)
    def _():
        up.wait_send()
        down.wait_recv()

    for f in range(2):
        spread(wide_one, f, 0, jnp.maximum(halo[0, f].astype(F32), 0.0))
        spread(wide_one, f, rows + 2, jnp.maximum(halo[1, f].astype(F32), 0.0))
    edges = [(f, r) for f in range(2) for r in (-1, rows - 1)]
    out = first(jnp.concatenate([taps(wide_one, f, r + 1, 2) for f, r in edges], axis=0))
    out = out.reshape(len(edges), 2, columns, channels)
    above = jnp.where(s > 0, 1.0, 0.0)
    below = jnp.where(s < strips - 1, 1.0, 0.0)
    for i, (f, r) in enumerate(edges):
        pair = [out[i, 0:1], out[i, 1:2]]
        if r < 0:
            pair[0] = pair[0] * above
        else:
            pair[1] = pair[1] * below
        spread(wide_two, f, r + 1, jnp.concatenate(pair, axis=0))
    edges = [(f, r) for f in range(2) for r in (0, rows - 2)]
    skip = jnp.concatenate(
        [maps[f, r : r + 2].reshape(2 * columns, channels).astype(F32) for f, r in edges], axis=0
    )
    out = second(jnp.concatenate([taps(wide_two, f, r, 2) for f, r in edges], axis=0), skip)
    for i, (f, r) in enumerate(edges):
        piece = out[2 * columns * i : 2 * columns * (i + 1)]
        block_ref[f, 0, r : r + 2] = piece.reshape(2, columns, channels)
        sums[f] = sums[f] + jnp.sum(piece, axis=0, keepdims=True)

    cells = rows * strips * columns
    lines = [total[:, LANES * p : LANES * (p + 1)] / cells for total in sums for p in range(packs)]
    blank = jnp.zeros((part.shape[0] - len(lines), LANES), F32)
    share = jnp.concatenate(lines + [blank], axis=0)
    part[...] = share
    parts[s] = share

    def part_copy(k):
        return pltpu.make_async_remote_copy(
            src_ref=part, dst_ref=parts.at[s],
            send_sem=part_send.at[k], recv_sem=part_recv.at[k],
            device_id=(b, lax.rem(s + k, strips)), device_id_type=MESH,
        )

    def note_copy(k):
        return pltpu.make_async_remote_copy(
            src_ref=note, dst_ref=notes.at[b],
            send_sem=note_send.at[k], recv_sem=note_recv.at[k],
            device_id=(lax.rem(b + k, batches), s), device_id_type=MESH,
        )

    def exchange(make, count):
        def start(k, carry):
            make(k).start()
            return carry

        def finish(k, carry):
            make(k).wait()
            return carry

        lax.fori_loop(1, count, start, 0)
        lax.fori_loop(1, count, finish, 0)

    exchange(part_copy, strips)
    pooled = jnp.sum(parts[...], axis=0)
    line = lax.broadcasted_iota(jnp.int32, pooled.shape, 0)
    pooled = jnp.where(line == 2 * packs, index_ref[0].astype(F32), pooled).astype(BF)
    note[...] = pooled
    notes[b] = pooled
    exchange(note_copy, batches)
    gathered_ref[...] = notes[...]
    loads[4].wait()
    loads[5].wait()


def unit_of(emb):
    inverse = lax.rsqrt(jnp.sum(emb * emb, axis=-1, keepdims=True) + 1e-06)
    return emb * inverse, inverse


def dot(left, right, over):
    return lax.dot_general(left, right, ((over[0:1], over[1:2]), ((), ())), preferred_element_type=F32)


def head_kernel(
    block_ref, gathered_ref, sproj_ref, gproj_ref, temp_ref,
    loss_ref, sgrad_ref, ggrad_ref, out_ref,
    sgrad, ggrad, sem,
):
    keep = pltpu.make_async_copy(block_ref, out_ref, sem.at[0])
    keep.start()
    batches = gathered_ref.shape[0]
    packs = sproj_ref.shape[0] // LANES
    heard = gathered_ref[...].astype(F32)

    def column(p):
        return jnp.concatenate([heard[i, p : p + 1] for i in range(batches)], axis=0)

    state_pool = jnp.concatenate([column(p) for p in range(packs)], axis=1).astype(BF)
    goal_pool = jnp.concatenate([column(packs + p) for p in range(packs)], axis=1).astype(BF)
    index = column(2 * packs)[:, 0:batches]
    sharpness = temp_ref[0]
    state_unit, state_inverse = unit_of(dot(state_pool, sproj_ref[...], (1, 0)))
    goal_unit, goal_inverse = unit_of(dot(goal_pool, gproj_ref[...], (1, 0)))
    state_bf = state_unit.astype(BF)
    goal_bf = goal_unit.astype(BF)
    logits = sharpness * dot(state_bf, goal_bf, (1, 1))
    exp_logits = jnp.exp(logits)
    row_total = jnp.sum(exp_logits, axis=1, keepdims=True)
    matched = lax.broadcasted_iota(jnp.int32, logits.shape, 1).astype(F32) == index
    positive = jnp.sum(jnp.where(matched, logits, 0.0), axis=1, keepdims=True)
    losses = jnp.log(row_total) - positive
    mine = lax.broadcasted_iota(jnp.int32, losses.shape, 0) == lax.axis_index("batch")
    loss_ref[0] = jnp.sum(jnp.where(mine, losses, 0.0))
    logit_grad = (exp_logits / row_total - matched.astype(F32)).astype(BF)
    copies = [keep]
    for i, (pool, unit, inverse, unit_grad, grad, target) in enumerate((
        (state_pool, state_unit, state_inverse, dot(logit_grad, goal_bf, (1, 0)), sgrad, sgrad_ref),
        (goal_pool, goal_unit, goal_inverse, dot(logit_grad, state_bf, (0, 0)), ggrad, ggrad_ref),
    )):
        unit_grad = sharpness * unit_grad
        along = jnp.sum(unit * unit_grad, axis=-1, keepdims=True)
        emb_grad = ((unit_grad - unit * along) * inverse).astype(BF)
        grad[...] = dot(pool, emb_grad, (0, 0))
        copies.append(pltpu.make_async_copy(grad, target, sem.at[1 + i]))
        copies[-1].start()
    for copy in copies:
        copy.wait()


def shards(batches, strips, state_maps, goal_maps, conv_one, conv_two, state_proj, goal_proj, inv_temp, pair_index):
    _, rows, columns, channels = state_maps.shape
    width = state_proj.shape[1]
    taps_in = conv_one.shape[0] * conv_one.shape[1] * channels
    any_spec = pl.BlockSpec(memory_space=pl.ANY)
    vmem = pl.BlockSpec(memory_space=pltpu.VMEM)
    smem = pl.BlockSpec(memory_space=pltpu.SMEM)
    block_shape = (2, 1, rows, columns, channels)
    dma = pltpu.SemaphoreType.DMA
    held = pl.pallas_call(
        functools.partial(block_kernel, batches, strips),
        out_shape=(
            pltpu.VMEM(block_shape, F32),
            pltpu.VMEM((batches, 8, LANES), BF),
            pltpu.VMEM((channels, width), BF),
            pltpu.VMEM((channels, width), BF),
        ),
        in_specs=[any_spec] * 6 + [smem],
        out_specs=(vmem, vmem, vmem, vmem),
        scratch_shapes=[
            pltpu.VMEM((2, rows, columns, channels), BF),
            pltpu.VMEM((2, rows + 4, columns, 3 * channels), BF),
            pltpu.VMEM((2, rows + 2, columns, 3 * channels), BF),
            pltpu.VMEM((taps_in, channels), BF),
            pltpu.VMEM((taps_in, channels), BF),
            pltpu.VMEM((2, 2, 2, columns, channels), BF),
            pltpu.VMEM((8, LANES), F32),
            pltpu.VMEM((strips, 8, LANES), F32),
            pltpu.VMEM((8, LANES), BF),
            pltpu.VMEM((batches, 8, LANES), BF),
            dma((6,)), dma((2,)), dma((2,)),
            dma((strips,)), dma((strips,)), dma((batches,)), dma((batches,)),
        ],
        compiler_params=pltpu.CompilerParams(
            collective_id=0, has_side_effects=True, vmem_limit_bytes=40 * 2**20
        ),
        name="block",
    )(
        state_maps, goal_maps,
        conv_one.reshape(taps_in, channels), conv_two.reshape(taps_in, channels),
        state_proj, goal_proj, pair_index,
    )
    held = [pltpu.with_memory_space_constraint(value, pltpu.VMEM) for value in held]
    return pl.pallas_call(
        head_kernel,
        out_shape=(
            jax.ShapeDtypeStruct((1,), F32),
            jax.ShapeDtypeStruct((channels, width), F32),
            jax.ShapeDtypeStruct((channels, width), F32),
            jax.ShapeDtypeStruct(block_shape, F32),
        ),
        in_specs=[vmem] * 4 + [smem],
        out_specs=(smem, any_spec, any_spec, any_spec),
        scratch_shapes=[
            pltpu.VMEM((channels, width), F32),
            pltpu.VMEM((channels, width), F32),
            dma((3,)),
        ],
        compiler_params=pltpu.CompilerParams(vmem_limit_bytes=40 * 2**20),
        name="head",
    )(*held, inv_temp)


def solution(mesh):
    placed = (
        P("batch", "strip", None, None),
        P("batch", "strip", None, None),
        P(),
        P(),
        P(),
        P(),
        P(),
        P("batch"),
    )
    return jax.shard_map(
        functools.partial(shards, mesh.shape["batch"], mesh.shape["strip"]),
        mesh=mesh,
        in_specs=placed,
        out_specs=(P("batch"), P(), P(), P(None, "batch", "strip", None, None)),
        check_vma=False,
    )
```

time: 285 us -> 30.2 us (0.11)
  blocking collectives: 119 us -> 0 us
  waiting for transfers between devices: 97.9 us -> 0 us
  Pallas kernels: 0 us -> 21.2 us
  between operations: 19.6 us -> 1.95 us
  other arithmetic: 13.4 us -> 0 us
  matrix products: 11.9 us -> 0 us
  starting transfers between devices: 8.23 us -> 0 us
  local copies, waits for them, and re-layouts: 14.3 us -> 6.7 us
    all_gather x3 -> x0, blocking collectives: 117 us -> none  [the longest x1 41.8 us: shards(): pool_piece = lax.all_gather(pool_pair, 'batch', axis=1, tiled=True)]
    unnamed x2 -> x0, waiting for transfers between devices: 96.3 us -> none
    pallas_call x0 -> x2, Pallas kernels: none -> 21.2 us  [the longest x1 18.3 us: shards(): pl.pallas_call(functools.partial(block_kernel, batches, strips), out_shap...]
    ppermute x4 -> x0, starting transfers between devices: 8.19 us -> none  [the longest x2 5.43 us: extended(): lax.ppermute(tail, axis, [(i, (i + 1) % count) for i in range(ends)])]
    conv_general_dilated x2 -> x0, matrix products: 6.02 us -> none  [conv_rows(): lax.conv_general_dilated(padded, kernel, (1, 1), ((0, 0), (1, 1)), dimens...]
    dot_general x6 -> x0, matrix products: 5.88 us -> none  [the longest x1 1.29 us: shards(): jnp.einsum('ic,ie->ce', pool_piece[1], grad_piece[1], preferred_element_t...]
    reduce_sum x4 -> x0, other arithmetic: 3.79 us -> none  [the longest x1 1.98 us: shards(): jnp.sum(goal_unit * goal_unit_grad, axis=-1, keepdims=True)]
    concatenate x3 -> x0, local copies, waits for them, and re-layouts: 3.4 us -> none  [the longest x2 2.06 us: extended(): jnp.concatenate([lax.ppermute(tail, axis, [(i, (i + 1) % count) for i in...]
  transfers between devices with their start and end apart: 5 -> 0, of which waited for: 2 -> 0; matrix products, arithmetic and copies ran while one was open for 2% -> 0% of each run, Pallas kernels for 0% -> 0%
where the time goes in v1:
time: 30.2 us; the launch traced here: 29.8 us
  Pallas kernels  21.2 us (70%)
  local copies, waits for them, and re-layouts  6.7 us (22%)
  between operations  1.95 us (6%)
    pallas_call x1, Pallas kernels, shards(): pl.pallas_call(functools.partial(block_kernel, batches, strips), out_shap...  18.3 us
    unnamed x12, local copies, waits for them, and re-layouts  6.7 us
    pallas_call x1, Pallas kernels, shards(): pl.pallas_call(head_kernel, out_shape=(jax.ShapeDtypeStruct((1,), F32), j...  2.92 us

profile of v1, /device:TPU:0, one launch (start us, length us, event | category | flops | bytes accessed | tf_op | source)
XLA Modules:
  0.0 29.8 jit_solution(8815429882812625345)
XLA Ops:
  1.9 0.0 copy-start
  1.9 1.3 %copy-done = bf16[3,3,256,256]{3,2,1,0:T(8,128)(2,1)S(1)} copy-done((bf16[3,3,256,256]{3,2,1,0:T(8,128)(2,1)S(1)}, bf16[3,3,256,256]{3,2,1,0:T(8,128)(2,1)}, u32[]{:S(2)}) %copy-start) | copy-done | bytes 1179672
  3.2 0.0 copy-start.1
  3.2 1.3 %copy-done.1 = bf16[3,3,256,256]{3,2,1,0:T(8,128)(2,1)S(1)} copy-done((bf16[3,3,256,256]{3,2,1,0:T(8,128)(2,1)S(1)}, bf16[3,3,256,256]{3,2,1,0:T(8,128)(2,1)}, u32[]{:S(2)}) %copy-start.1) | copy-done | bytes 1179672
  4.5 0.0 copy-start.2
  4.5 1.0 %copy-done.2 = bf16[1,16,64,256]{3,2,1,0:T(8,128)(2,1)S(1)} copy-done((bf16[1,16,64,256]{3,2,1,0:T(8,128)(2,1)S(1)}, bf16[1,16,64,256]{3,2,1,0:T(8,128)(2,1)}, u32[]{:S(2)}) %copy-start.2) | copy-done | bytes 524312
  5.5 0.0 copy-start.3
  5.5 1.0 %copy-done.3 = bf16[1,16,64,256]{3,2,1,0:T(8,128)(2,1)S(1)} copy-done((bf16[1,16,64,256]{3,2,1,0:T(8,128)(2,1)S(1)}, bf16[1,16,64,256]{3,2,1,0:T(8,128)(2,1)}, u32[]{:S(2)}) %copy-start.3) | copy-done | bytes 524312
  6.6 0.0 copy-start.4
  6.6 1.0 %copy-done.4 = bf16[256,1024]{1,0:T(8,128)(2,1)S(1)} copy-done((bf16[256,1024]{1,0:T(8,128)(2,1)S(1)}, bf16[256,1024]{1,0:T(8,128)(2,1)}, u32[]{:S(2)}) %copy-start.4) | copy-done | bytes 524312
  7.6 0.0 copy-start.5
  7.6 1.0 %copy-done.5 = bf16[256,1024]{1,0:T(8,128)(2,1)S(1)} copy-done((bf16[256,1024]{1,0:T(8,128)(2,1)S(1)}, bf16[256,1024]{1,0:T(8,128)(2,1)}, u32[]{:S(2)}) %copy-start.5) | copy-done | bytes 524312
  8.6 18.3 %block.1 = (f32[2,1,16,64,256]{4,3,2,1,0:T(8,128)S(1)}, bf16[16,8,128]{2,1,0:T(8,128)(2,1)S(1)}, bf16[256,1024]{1,0:T(8,128)(2,1)S(1)}, bf16[256,1024]{1,0:T(8,128)(2,1)S(1)}) custom-call(bf16[1,16,64,256]{3,2,1,0:T(8,128)(2,1)S(1)} %copy-done.2, bf16[1,16,64,256]{3,2,1,0:T(8,128)(2,1)S(1)} %copy-done.3, bf16[2304,256]{1,0:T(8,128)(2,1)S(1)} %bitcast.2, ...), custom_call_target="tpu_custom_call" | custom-call | tf_op jit(solution)/shard_map/block/pallas_call | solution.py:271
  26.9 2.9 %head.1 = (f32[1]{0:T(128)}, f32[256,1024]{1,0:T(8,128)}, f32[256,1024]{1,0:T(8,128)}, f32[2,1,16,64,256]{4,3,2,1,0:T(8,128)}) custom-call(f32[2,1,16,64,256]{4,3,2,1,0:T(8,128)S(1)} %get-tuple-element.8.block_ref, bf16[16,8,128]{2,1,0:T(8,128)(2,1)S(1)} %get-tuple-element.9.gathered_ref, bf16[256,1024]{1,0:T(8,128)(2,1)S(1)} %get-tuple-element.10.sproj_ref, ...), custom_call_target="tpu_custom_call" | custom-call | tf_op jit(solution)/shard_map/head/pallas_call | solution.py:305
Async XLA Ops:
  1.9 1.3 %copy-start = (bf16[3,3,256,256]{3,2,1,0:T(8,128)(2,1)S(1)}, bf16[3,3,256,256]{3,2,1,0:T(8,128)(2,1)}, u32[]{:S(2)}) copy-start(bf16[3,3,256,256]{3,2,1,0:T(8,128)(2,1)} %param.10) | copy-start | bytes 3538948
  3.2 1.3 %copy-start.1 = (bf16[3,3,256,256]{3,2,1,0:T(8,128)(2,1)S(1)}, bf16[3,3,256,256]{3,2,1,0:T(8,128)(2,1)}, u32[]{:S(2)}) copy-start(bf16[3,3,256,256]{3,2,1,0:T(8,128)(2,1)} %param.11) | copy-start | bytes 3538948
  4.5 1.0 %copy-start.2 = (bf16[1,16,64,256]{3,2,1,0:T(8,128)(2,1)S(1)}, bf16[1,16,64,256]{3,2,1,0:T(8,128)(2,1)}, u32[]{:S(2)}) copy-start(bf16[1,16,64,256]{3,2,1,0:T(8,128)(2,1)} %state_ref.1) | copy-start | bytes 1572868
  5.5 1.0 %copy-start.3 = (bf16[1,16,64,256]{3,2,1,0:T(8,128)(2,1)S(1)}, bf16[1,16,64,256]{3,2,1,0:T(8,128)(2,1)}, u32[]{:S(2)}) copy-start(bf16[1,16,64,256]{3,2,1,0:T(8,128)(2,1)} %goal_ref.1) | copy-start | bytes 1572868
  6.6 1.0 %copy-start.4 = (bf16[256,1024]{1,0:T(8,128)(2,1)S(1)}, bf16[256,1024]{1,0:T(8,128)(2,1)}, u32[]{:S(2)}) copy-start(bf16[256,1024]{1,0:T(8,128)(2,1)} %sproj_ref.1) | copy-start | bytes 1572868
  7.6 1.0 %copy-start.5 = (bf16[256,1024]{1,0:T(8,128)(2,1)S(1)}, bf16[256,1024]{1,0:T(8,128)(2,1)}, u32[]{:S(2)}) copy-start(bf16[256,1024]{1,0:T(8,128)(2,1)} %gproj_ref.1) | copy-start | bytes 1572868

commit v2 on v1

--- a/solution.py
+++ b/solution.py
@@ -268,6 +268,14 @@
     smem = pl.BlockSpec(memory_space=pltpu.SMEM)
     block_shape = (2, 1, rows, columns, channels)
     dma = pltpu.SemaphoreType.DMA
+    stay = [
+        pltpu.with_memory_space_constraint(value, pltpu.HBM)
+        for value in (
+            state_maps, goal_maps,
+            conv_one.reshape(taps_in, channels), conv_two.reshape(taps_in, channels),
+            state_proj, goal_proj,
+        )
+    ]
     held = pl.pallas_call(
         functools.partial(block_kernel, batches, strips),
         out_shape=(
@@ -296,11 +304,7 @@
             collective_id=0, has_side_effects=True, vmem_limit_bytes=40 * 2**20
         ),
         name="block",
-    )(
-        state_maps, goal_maps,
-        conv_one.reshape(taps_in, channels), conv_two.reshape(taps_in, channels),
-        state_proj, goal_proj, pair_index,
-    )
+    )(*stay, pair_index)
     held = [pltpu.with_memory_space_constraint(value, pltpu.VMEM) for value in held]
     return pl.pallas_call(
         head_kernel,

time: 30.2 us -> 23.6 us (0.78)
  local copies, waits for them, and re-layouts: 6.7 us -> 0 us
    unnamed x12 -> x0, local copies, waits for them, and re-layouts: 6.7 us -> none
    pallas_call x1, Pallas kernels: 18.3 us -> 18.6 us  [shards(): pl.pallas_call(functools.partial(block_kernel, batches, strips), out_shap...]
where the time goes in v2:
time: 23.6 us; the launch traced here: 23.4 us
  Pallas kernels  21.5 us (91%)
  between operations  1.93 us (8%)
    pallas_call x1, Pallas kernels, shards(): pl.pallas_call(functools.partial(block_kernel, batches, strips), out_shap...  18.6 us
    pallas_call x1, Pallas kernels, shards(): pl.pallas_call(head_kernel, out_shape=(jax.ShapeDtypeStruct((1,), F32), j...  2.91 us

profile of v2, /device:TPU:0, one launch (start us, length us, event | category | flops | bytes accessed | tf_op | source)
XLA Modules:
  0.0 23.4 jit_solution(17272025472862544463)
XLA Ops:
  1.9 18.6 %block.1 = (f32[2,1,16,64,256]{4,3,2,1,0:T(8,128)S(1)}, bf16[16,8,128]{2,1,0:T(8,128)(2,1)S(1)}, bf16[256,1024]{1,0:T(8,128)(2,1)S(1)}, bf16[256,1024]{1,0:T(8,128)(2,1)S(1)}) custom-call(bf16[1,16,64,256]{3,2,1,0:T(8,128)(2,1)} %state_ref.1, bf16[1,16,64,256]{3,2,1,0:T(8,128)(2,1)} %goal_ref.1, bf16[2304,256]{1,0:T(8,128)(2,1)} %bitcast.2, ...), custom_call_target="tpu_custom_call" | custom-call | tf_op jit(solution)/shard_map/block/pallas_call | solution.py:279
  20.5 2.9 %head.1 = (f32[1]{0:T(128)}, f32[256,1024]{1,0:T(8,128)}, f32[256,1024]{1,0:T(8,128)}, f32[2,1,16,64,256]{4,3,2,1,0:T(8,128)}) custom-call(f32[2,1,16,64,256]{4,3,2,1,0:T(8,128)S(1)} %get-tuple-element.8.block_ref, bf16[16,8,128]{2,1,0:T(8,128)(2,1)S(1)} %get-tuple-element.9.gathered_ref, bf16[256,1024]{1,0:T(8,128)(2,1)S(1)} %get-tuple-element.10.sproj_ref, ...), custom_call_target="tpu_custom_call" | custom-call | tf_op jit(solution)/shard_map/head/pallas_call | solution.py:309

commit v3 on v2

v3 whole, which is shorter than its diff:
```python
import functools

import jax
import jax.numpy as jnp
from jax import lax
from jax.experimental import pallas as pl
from jax.experimental.pallas import tpu as pltpu
from jax.sharding import PartitionSpec as P

MESH = pl.DeviceIdType.MESH
BF = jnp.bfloat16
F32 = jnp.float32
LANES = 128


def spread(dst, frame, row, cells):
    rows, columns, channels = cells.shape
    where = lax.broadcasted_iota(jnp.int32, cells.shape, 1)
    left = jnp.where(where == 0, 0.0, pltpu.roll(cells, 1, axis=1))
    right = jnp.where(where == columns - 1, 0.0, pltpu.roll(cells, columns - 1, axis=1))
    span = pl.ds(row, rows)
    dst[frame, span, :, 0:channels] = left.astype(BF)
    dst[frame, span, :, channels : 2 * channels] = cells.astype(BF)
    dst[frame, span, :, 2 * channels : 3 * channels] = right.astype(BF)


def taps(src, frame, row, rows):
    columns, width = src.shape[2], src.shape[3]
    return jnp.concatenate(
        [src[frame, row + d : row + d + rows].reshape(rows * columns, width) for d in range(3)],
        axis=1,
    )


def block_kernel(
    batches, strips,
    state_ref, goal_ref, one_ref, two_ref, sproj_ref, gproj_ref, index_ref,
    block_ref, gathered_ref, marks_out, sproj_out, gproj_out,
    maps, wide_one, wide_two, w_one, w_two, halo, mark, marks, part, parts, note, notes,
    load_sem, halo_send, halo_recv,
    mark_send, mark_recv, part_send, part_recv, note_send, note_recv,
):
    b = lax.axis_index("batch")
    s = lax.axis_index("strip")
    rows, columns, channels = maps.shape[1], maps.shape[2], maps.shape[3]
    packs = channels // LANES

    loads = [
        pltpu.make_async_copy(source, target, load_sem.at[i])
        for i, (source, target) in enumerate((
            (state_ref.at[0], maps.at[0]),
            (goal_ref.at[0], maps.at[1]),
            (one_ref, w_one),
            (two_ref, w_two),
            (sproj_ref, sproj_out),
            (gproj_ref, gproj_out),
        ))
    ]
    for copy in loads:
        copy.start()

    @pl.when(s == 0)
    def _():
        halo[0] = jnp.zeros(halo.shape[1:], BF)

    @pl.when(s == strips - 1)
    def _():
        halo[1] = jnp.zeros(halo.shape[1:], BF)

    mark[...] = jnp.full(mark.shape, index_ref[0].astype(F32))
    marks[b] = mark[...]
    barrier = pltpu.get_barrier_semaphore()

    def greet_strip(k, carry):
        pl.semaphore_signal(barrier, inc=1, device_id=(b, lax.rem(s + k, strips)), device_id_type=MESH)
        return carry

    def greet_batch(k, carry):
        pl.semaphore_signal(barrier, inc=1, device_id=(lax.rem(b + k, batches), s), device_id_type=MESH)
        return carry

    lax.fori_loop(1, batches, greet_batch, 0)
    lax.fori_loop(1, strips, greet_strip, 0)

    def part_copy(k):
        return pltpu.make_async_remote_copy(
            src_ref=part, dst_ref=parts.at[s],
            send_sem=part_send.at[k], recv_sem=part_recv.at[k],
            device_id=(b, lax.rem(s + k, strips)), device_id_type=MESH,
        )

    def note_copy(k):
        return pltpu.make_async_remote_copy(
            src_ref=note, dst_ref=notes.at[b],
            send_sem=note_send.at[k], recv_sem=note_recv.at[k],
            device_id=(lax.rem(b + k, batches), s), device_id_type=MESH,
        )

    def mark_copy(k):
        return pltpu.make_async_remote_copy(
            src_ref=mark, dst_ref=marks.at[b],
            send_sem=mark_send.at[k], recv_sem=mark_recv.at[k],
            device_id=(lax.rem(b + k, batches), s), device_id_type=MESH,
        )

    def start(make, count):
        def one(k, carry):
            make(k).start()
            return carry

        lax.fori_loop(1, count, one, 0)

    def finish(make, count):
        def one(k, carry):
            make(k).wait()
            return carry

        lax.fori_loop(1, count, one, 0)

    loads[0].wait()
    spread(wide_one, 0, 2, jnp.maximum(maps[0].astype(F32), 0.0))
    loads[1].wait()
    pl.semaphore_wait(barrier, strips + batches - 2)
    down = pltpu.make_async_remote_copy(
        src_ref=maps.at[:, rows - 2 : rows], dst_ref=halo.at[0],
        send_sem=halo_send.at[0], recv_sem=halo_recv.at[0],
        device_id=(b, lax.rem(s + 1, strips)), device_id_type=MESH,
    )
    up = pltpu.make_async_remote_copy(
        src_ref=maps.at[:, 0:2], dst_ref=halo.at[1],
        send_sem=halo_send.at[1], recv_sem=halo_recv.at[1],
        device_id=(b, lax.rem(s + strips - 1, strips)), device_id_type=MESH,
    )

    @pl.when(s < strips - 1)
    def _():
        down.start()

    @pl.when(s > 0)
    def _():
        up.start()

    start(mark_copy, batches)

    above = jnp.where(s > 0, 1.0, 0.0)
    below = jnp.where(s < strips - 1, 1.0, 0.0)

    def first(pieces):
        lhs = [taps(wide_one, f, r + 1, count) for f, r, count in pieces]
        lhs = lhs[0] if len(lhs) == 1 else jnp.concatenate(lhs, axis=0)
        out = jnp.maximum(jnp.dot(lhs, w_one[...], preferred_element_type=F32), 0.0)
        at = 0
        for f, r, count in pieces:
            piece = out[at : at + count * columns].reshape(count, columns, channels)
            at += count * columns
            if r < 0:
                piece = jnp.concatenate([piece[0:1] * above, piece[1:]], axis=0)
            if r + count > rows:
                piece = jnp.concatenate([piece[: count - 1], piece[count - 1 :] * below], axis=0)
            spread(wide_two, f, r + 1, piece)

    spread(wide_one, 1, 2, jnp.maximum(maps[1].astype(F32), 0.0))
    loads[2].wait()
    half = (rows - 2) // 2
    for r in range(1, rows - 1, half):
        first([(0, r, half)])

    loads[3].wait()

    @pl.when(s < strips - 1)
    def _():
        down.wait_send()
        up.wait_recv()

    @pl.when(s > 0)
    def _():
        up.wait_send()
        down.wait_recv()

    for f in range(2):
        spread(wide_one, f, 0, jnp.maximum(halo[0, f].astype(F32), 0.0))
        spread(wide_one, f, rows + 2, jnp.maximum(halo[1, f].astype(F32), 0.0))
    first([(0, -1, 2), (0, rows - 1, 2)])
    half = (rows + 2) // 2
    for r in range(-1, rows + 1, half):
        first([(1, r, half)])
    sums = []
    half = rows // 2
    for f in range(2):
        total = jnp.zeros((1, channels), F32)
        for r in range(0, rows, half):
            skip = maps[f, r : r + half].reshape(half * columns, channels).astype(F32)
            out = jnp.dot(taps(wide_two, f, r, half), w_two[...], preferred_element_type=F32)
            out = jnp.maximum(skip + out, 0.0)
            block_ref[f, 0, r : r + half] = out.reshape(half, columns, channels)
            total = total + jnp.sum(out, axis=0, keepdims=True)
        sums.append(total)

    cells = rows * strips * columns
    lines = [total[:, LANES * p : LANES * (p + 1)] / cells for total in sums for p in range(packs)]
    share = jnp.concatenate(lines, axis=0)
    part[...] = share
    parts[s] = share
    start(part_copy, strips)
    finish(part_copy, strips)
    pooled = jnp.sum(parts[...], axis=0).astype(BF)
    note[...] = pooled
    notes[b] = pooled
    start(note_copy, batches)
    finish(mark_copy, batches)
    marks_out[...] = jnp.concatenate([marks[i, 0:1] for i in range(batches)], axis=0)
    finish(note_copy, batches)
    gathered_ref[...] = notes[...]
    loads[4].wait()
    loads[5].wait()


def unit_of(emb):
    inverse = lax.rsqrt(jnp.sum(emb * emb, axis=-1, keepdims=True) + 1e-06)
    return emb * inverse, inverse


def dot(left, right, over):
    return lax.dot_general(left, right, ((over[0:1], over[1:2]), ((), ())), preferred_element_type=F32)


def head_kernel(
    block_ref, gathered_ref, marks_ref, sproj_ref, gproj_ref, temp_ref,
    loss_ref, sgrad_ref, ggrad_ref, out_ref,
    sgrad, ggrad, sem,
):
    keep = pltpu.make_async_copy(block_ref, out_ref, sem.at[0])
    keep.start()
    batches = gathered_ref.shape[0]
    packs = sproj_ref.shape[0] // LANES
    heard = gathered_ref[...].astype(F32)

    def column(p):
        return jnp.concatenate([heard[i, p : p + 1] for i in range(batches)], axis=0)

    state_pool = jnp.concatenate([column(p) for p in range(packs)], axis=1).astype(BF)
    goal_pool = jnp.concatenate([column(packs + p) for p in range(packs)], axis=1).astype(BF)
    index = marks_ref[:, 0:batches]
    sharpness = temp_ref[0]
    state_unit, state_inverse = unit_of(dot(state_pool, sproj_ref[...], (1, 0)))
    goal_unit, goal_inverse = unit_of(dot(goal_pool, gproj_ref[...], (1, 0)))
    state_bf = state_unit.astype(BF)
    goal_bf = goal_unit.astype(BF)
    logits = sharpness * dot(state_bf, goal_bf, (1, 1))
    exp_logits = jnp.exp(logits)
    row_total = jnp.sum(exp_logits, axis=1, keepdims=True)
    matched = lax.broadcasted_iota(jnp.int32, logits.shape, 1).astype(F32) == index
    positive = jnp.sum(jnp.where(matched, logits, 0.0), axis=1, keepdims=True)
    losses = jnp.log(row_total) - positive
    mine = lax.broadcasted_iota(jnp.int32, losses.shape, 0) == lax.axis_index("batch")
    loss_ref[0] = jnp.sum(jnp.where(mine, losses, 0.0))
    logit_grad = (exp_logits / row_total - matched.astype(F32)).astype(BF)
    copies = [keep]
    for i, (pool, unit, inverse, unit_grad, grad, target) in enumerate((
        (state_pool, state_unit, state_inverse, dot(logit_grad, goal_bf, (1, 0)), sgrad, sgrad_ref),
        (goal_pool, goal_unit, goal_inverse, dot(logit_grad, state_bf, (0, 0)), ggrad, ggrad_ref),
    )):
        unit_grad = sharpness * unit_grad
        along = jnp.sum(unit * unit_grad, axis=-1, keepdims=True)
        emb_grad = ((unit_grad - unit * along) * inverse).astype(BF)
        grad[...] = dot(pool, emb_grad, (0, 0))
        copies.append(pltpu.make_async_copy(grad, target, sem.at[1 + i]))
        copies[-1].start()
    for copy in copies:
        copy.wait()


def shards(batches, strips, state_maps, goal_maps, conv_one, conv_two, state_proj, goal_proj, inv_temp, pair_index):
    _, rows, columns, channels = state_maps.shape
    width = state_proj.shape[1]
    taps_in = conv_one.shape[0] * conv_one.shape[1] * channels
    any_spec = pl.BlockSpec(memory_space=pl.ANY)
    vmem = pl.BlockSpec(memory_space=pltpu.VMEM)
    smem = pl.BlockSpec(memory_space=pltpu.SMEM)
    block_shape = (2, 1, rows, columns, channels)
    dma = pltpu.SemaphoreType.DMA
    lines = 2 * channels // LANES
    stay = [
        pltpu.with_memory_space_constraint(value, pltpu.HBM)
        for value in (
            state_maps, goal_maps,
            conv_one.reshape(taps_in, channels), conv_two.reshape(taps_in, channels),
            state_proj, goal_proj,
        )
    ]
    held = pl.pallas_call(
        functools.partial(block_kernel, batches, strips),
        out_shape=(
            pltpu.VMEM(block_shape, F32),
            pltpu.VMEM((batches, lines, LANES), BF),
            pltpu.VMEM((batches, LANES), F32),
            pltpu.VMEM((channels, width), BF),
            pltpu.VMEM((channels, width), BF),
        ),
        in_specs=[any_spec] * 6 + [smem],
        out_specs=(vmem,) * 5,
        scratch_shapes=[
            pltpu.VMEM((2, rows, columns, channels), BF),
            pltpu.VMEM((2, rows + 4, columns, 3 * channels), BF),
            pltpu.VMEM((2, rows + 2, columns, 3 * channels), BF),
            pltpu.VMEM((taps_in, channels), BF),
            pltpu.VMEM((taps_in, channels), BF),
            pltpu.VMEM((2, 2, 2, columns, channels), BF),
            pltpu.VMEM((8, LANES), F32),
            pltpu.VMEM((batches, 8, LANES), F32),
            pltpu.VMEM((lines, LANES), F32),
            pltpu.VMEM((strips, lines, LANES), F32),
            pltpu.VMEM((lines, LANES), BF),
            pltpu.VMEM((batches, lines, LANES), BF),
            dma((6,)), dma((2,)), dma((2,)), dma((batches,)), dma((batches,)),
            dma((strips,)), dma((strips,)), dma((batches,)), dma((batches,)),
        ],
        compiler_params=pltpu.CompilerParams(
            collective_id=0, has_side_effects=True, vmem_limit_bytes=40 * 2**20
        ),
        name="block",
    )(*stay, pair_index)
    held = [pltpu.with_memory_space_constraint(value, pltpu.VMEM) for value in held]
    return pl.pallas_call(
        head_kernel,
        out_shape=(
            jax.ShapeDtypeStruct((1,), F32),
            jax.ShapeDtypeStruct((channels, width), F32),
            jax.ShapeDtypeStruct((channels, width), F32),
            jax.ShapeDtypeStruct(block_shape, F32),
        ),
        in_specs=[vmem] * 5 + [smem],
        out_specs=(smem, any_spec, any_spec, any_spec),
        scratch_shapes=[
            pltpu.VMEM((channels, width), F32),
            pltpu.VMEM((channels, width), F32),
            dma((3,)),
        ],
        compiler_params=pltpu.CompilerParams(vmem_limit_bytes=40 * 2**20),
        name="head",
    )(*held, inv_temp)


def solution(mesh):
    placed = (
        P("batch", "strip", None, None),
        P("batch", "strip", None, None),
        P(),
        P(),
        P(),
        P(),
        P(),
        P("batch"),
    )
    return jax.shard_map(
        functools.partial(shards, mesh.shape["batch"], mesh.shape["strip"]),
        mesh=mesh,
        in_specs=placed,
        out_specs=(P("batch"), P(), P(), P(None, "batch", "strip", None, None)),
        check_vma=False,
    )
```

time: 23.6 us -> 22.6 us (0.958)
  Pallas kernels: 21.5 us -> 20.5 us
    pallas_call x1, Pallas kernels: 18.6 us -> 17.6 us  [shards(): pl.pallas_call(functools.partial(block_kernel, batches, strips), out_shap...]
where the time goes in v3:
time: 22.6 us; the launch traced here: 22.4 us
  Pallas kernels  20.5 us (91%)
  between operations  1.93 us (9%)
    pallas_call x1, Pallas kernels, shards(): pl.pallas_call(functools.partial(block_kernel, batches, strips), out_shap...  17.6 us
    pallas_call x1, Pallas kernels, shards(): pl.pallas_call(head_kernel, out_shape=(jax.ShapeDtypeStruct((1,), F32), j...  2.92 us

profile of v3, /device:TPU:0, one launch (start us, length us, event | category | flops | bytes accessed | tf_op | source)
XLA Modules:
  0.0 22.4 jit_solution(12655126741693000484)
XLA Ops:
  1.9 17.6 %block.1 = (f32[2,1,16,64,256]{4,3,2,1,0:T(8,128)S(1)}, bf16[16,4,128]{2,1,0:T(4,128)(2,1)S(1)}, f32[16,128]{1,0:T(8,128)S(1)}, bf16[256,1024]{1,0:T(8,128)(2,1)S(1)}, bf16[256,1024]{1,0:T(8,128)(2,1)S(1)}) custom-call(bf16[1,16,64,256]{3,2,1,0:T(8,128)(2,1)} %state_ref.1, bf16[1,16,64,256]{3,2,1,0:T(8,128)(2,1)} %goal_ref.1, bf16[2304,256]{1,0:T(8,128)(2,1)} %bitcast.2, ...), custom_call_target="tpu_custom_call" | custom-call | tf_op jit(solution)/shard_map/block/pallas_call | solution.py:291
  19.5 2.9 %head.1 = (f32[1]{0:T(128)}, f32[256,1024]{1,0:T(8,128)}, f32[256,1024]{1,0:T(8,128)}, f32[2,1,16,64,256]{4,3,2,1,0:T(8,128)}) custom-call(f32[2,1,16,64,256]{4,3,2,1,0:T(8,128)S(1)} %get-tuple-element.9.block_ref, bf16[16,4,128]{2,1,0:T(4,128)(2,1)S(1)} %get-tuple-element.10.gathered_ref, f32[16,128]{1,0:T(8,128)S(1)} %get-tuple-element.11.marks_ref, ...), custom_call_target="tpu_custom_call" | custom-call | tf_op jit(solution)/shard_map/head/pallas_call | solution.py:324

commit v4 on v3

--- a/solution.py
+++ b/solution.py
@@ -11,6 +11,7 @@
 BF = jnp.bfloat16
 F32 = jnp.float32
 LANES = 128
+ROWS_AT_ONCE = 6
 
 
 def spread(dst, frame, row, cells):
@@ -22,6 +23,12 @@
     dst[frame, span, :, 0:channels] = left.astype(BF)
     dst[frame, span, :, channels : 2 * channels] = cells.astype(BF)
     dst[frame, span, :, 2 * channels : 3 * channels] = right.astype(BF)
+
+
+def chunks(start, stop):
+    number = -(-(stop - start) // ROWS_AT_ONCE)
+    cuts = [start + (stop - start) * i // number for i in range(number + 1)]
+    return [(low, high - low) for low, high in zip(cuts, cuts[1:])]
 
 
 def taps(src, frame, row, rows):
@@ -67,8 +74,6 @@
     def _():
         halo[1] = jnp.zeros(halo.shape[1:], BF)
 
-    mark[...] = jnp.full(mark.shape, index_ref[0].astype(F32))
-    marks[b] = mark[...]
     barrier = pltpu.get_barrier_semaphore()
 
     def greet_strip(k, carry):
@@ -119,6 +124,9 @@
 
     loads[0].wait()
     spread(wide_one, 0, 2, jnp.maximum(maps[0].astype(F32), 0.0))
+    told = jnp.full(mark.shape, index_ref[0].astype(F32))
+    mark[...] = told
+    marks[b] = told
     loads[1].wait()
     pl.semaphore_wait(barrier, strips + batches - 2)
     down = pltpu.make_async_remote_copy(
@@ -161,9 +169,8 @@
 
     spread(wide_one, 1, 2, jnp.maximum(maps[1].astype(F32), 0.0))
     loads[2].wait()
-    half = (rows - 2) // 2
-    for r in range(1, rows - 1, half):
-        first([(0, r, half)])
+    for r, count in chunks(1, rows - 1):
+        first([(0, r, count)])
 
     loads[3].wait()
 
@@ -181,18 +188,16 @@
         spread(wide_one, f, 0, jnp.maximum(halo[0, f].astype(F32), 0.0))
         spread(wide_one, f, rows + 2, jnp.maximum(halo[1, f].astype(F32), 0.0))
     first([(0, -1, 2), (0, rows - 1, 2)])
-    half = (rows + 2) // 2
-    for r in range(-1, rows + 1, half):
-        first([(1, r, half)])
+    for r, count in chunks(-1, rows + 1):
+        first([(1, r, count)])
     sums = []
-    half = rows // 2
     for f in range(2):
         total = jnp.zeros((1, channels), F32)
-        for r in range(0, rows, half):
-            skip = maps[f, r : r + half].reshape(half * columns, channels).astype(F32)
-            out = jnp.dot(taps(wide_two, f, r, half), w_two[...], preferred_element_type=F32)
+        for r, count in chunks(0, rows):
+            skip = maps[f, r : r + count].reshape(count * columns, channels).astype(F32)
+            out = jnp.dot(taps(wide_two, f, r, count), w_two[...], preferred_element_type=F32)
             out = jnp.maximum(skip + out, 0.0)
-            block_ref[f, 0, r : r + half] = out.reshape(half, columns, channels)
+            block_ref[f, 0, r : r + count] = out.reshape(count, columns, channels)
             total = total + jnp.sum(out, axis=0, keepdims=True)
         sums.append(total)
 
@@ -227,7 +232,7 @@
 def head_kernel(
     block_ref, gathered_ref, marks_ref, sproj_ref, gproj_ref, temp_ref,
     loss_ref, sgrad_ref, ggrad_ref, out_ref,
-    sgrad, ggrad, sem,
+    loss, sgrad, ggrad, sem,
 ):
     keep = pltpu.make_async_copy(block_ref, out_ref, sem.at[0])
     keep.start()
@@ -253,19 +258,23 @@
     positive = jnp.sum(jnp.where(matched, logits, 0.0), axis=1, keepdims=True)
     losses = jnp.log(row_total) - positive
     mine = lax.broadcasted_iota(jnp.int32, losses.shape, 0) == lax.axis_index("batch")
-    loss_ref[0] = jnp.sum(jnp.where(mine, losses, 0.0))
+    loss[0] = jnp.sum(jnp.where(mine, losses, 0.0))
+    say = pltpu.make_async_copy(loss, loss_ref, sem.at[1])
+    say.start()
     logit_grad = (exp_logits / row_total - matched.astype(F32)).astype(BF)
-    copies = [keep]
-    for i, (pool, unit, inverse, unit_grad, grad, target) in enumerate((
+    copies = [keep, say]
+    for pool, unit, inverse, unit_grad, grad, target in (
         (state_pool, state_unit, state_inverse, dot(logit_grad, goal_bf, (1, 0)), sgrad, sgrad_ref),
         (goal_pool, goal_unit, goal_inverse, dot(logit_grad, state_bf, (0, 0)), ggrad, ggrad_ref),
-    )):
+    ):
         unit_grad = sharpness * unit_grad
         along = jnp.sum(unit * unit_grad, axis=-1, keepdims=True)
         emb_grad = ((unit_grad - unit * along) * inverse).astype(BF)
-        grad[...] = dot(pool, emb_grad, (0, 0))
-        copies.append(pltpu.make_async_copy(grad, target, sem.at[1 + i]))
-        copies[-1].start()
+        for p in range(packs):
+            span = slice(LANES * p, LANES * (p + 1))
+            grad[span] = dot(pool[:, span], emb_grad, (0, 0))
+            copies.append(pltpu.make_async_copy(grad.at[span], target.at[span], sem.at[len(copies)]))
+            copies[-1].start()
     for copy in copies:
         copy.wait()
 
@@ -275,8 +284,8 @@
     width = state_proj.shape[1]
     taps_in = conv_one.shape[0] * conv_one.shape[1] * channels
     any_spec = pl.BlockSpec(memory_space=pl.ANY)
+    smem = pl.BlockSpec(memory_space=pltpu.SMEM)
     vmem = pl.BlockSpec(memory_space=pltpu.VMEM)
-    smem = pl.BlockSpec(memory_space=pltpu.SMEM)
     block_shape = (2, 1, rows, columns, channels)
     dma = pltpu.SemaphoreType.DMA
     lines = 2 * channels // LANES
@@ -330,11 +339,12 @@
             jax.ShapeDtypeStruct(block_shape, F32),
         ),
         in_specs=[vmem] * 5 + [smem],
-        out_specs=(smem, any_spec, any_spec, any_spec),
+        out_specs=(any_spec,) * 4,
         scratch_shapes=[
+            pltpu.SMEM((1,), F32),
             pltpu.VMEM((channels, width), F32),
             pltpu.VMEM((channels, width), F32),
-            dma((3,)),
+            dma((2 + 2 * (channels // LANES),)),
         ],
         compiler_params=pltpu.CompilerParams(vmem_limit_bytes=40 * 2**20),
         name="head",

time: 22.6 us -> 22.5 us (level)
    pallas_call x1, Pallas kernels: 2.92 us -> 2.37 us  [shards(): pl.pallas_call(head_kernel, out_shape=(jax.ShapeDtypeStruct((1,), F32), j...]
    pallas_call x1, Pallas kernels: 17.6 us -> 18.1 us  [shards(): pl.pallas_call(functools.partial(block_kernel, batches, strips), out_shap...]
where the time goes in v4:
time: 22.5 us; the launch traced here: 22.4 us
  Pallas kernels  20.4 us (91%)
  between operations  1.93 us (9%)
    pallas_call x1, Pallas kernels, shards(): pl.pallas_call(functools.partial(block_kernel, batches, strips), out_shap...  18.1 us
    pallas_call x1, Pallas kernels, shards(): pl.pallas_call(head_kernel, out_shape=(jax.ShapeDtypeStruct((1,), F32), j...  2.37 us

profile of v4, /device:TPU:0, one launch (start us, length us, event | category | flops | bytes accessed | tf_op | source)
XLA Modules:
  0.0 22.4 jit_solution(5754709563438857209)
XLA Ops:
  1.9 18.1 %block.1 = (f32[2,1,16,64,256]{4,3,2,1,0:T(8,128)S(1)}, bf16[16,4,128]{2,1,0:T(4,128)(2,1)S(1)}, f32[16,128]{1,0:T(8,128)S(1)}, bf16[256,1024]{1,0:T(8,128)(2,1)S(1)}, bf16[256,1024]{1,0:T(8,128)(2,1)S(1)}) custom-call(bf16[1,16,64,256]{3,2,1,0:T(8,128)(2,1)} %state_ref.1, bf16[1,16,64,256]{3,2,1,0:T(8,128)(2,1)} %goal_ref.1, bf16[2304,256]{1,0:T(8,128)(2,1)} %bitcast.2, ...), custom_call_target="tpu_custom_call" | custom-call | tf_op jit(solution)/shard_map/block/pallas_call | solution.py:300
  20.0 2.4 %head.1 = (f32[1]{0:T(128)}, f32[256,1024]{1,0:T(8,128)}, f32[256,1024]{1,0:T(8,128)}, f32[2,1,16,64,256]{4,3,2,1,0:T(8,128)}) custom-call(f32[2,1,16,64,256]{4,3,2,1,0:T(8,128)S(1)} %get-tuple-element.9.block_ref, bf16[16,4,128]{2,1,0:T(4,128)(2,1)S(1)} %get-tuple-element.10.gathered_ref, f32[16,128]{1,0:T(8,128)S(1)} %get-tuple-element.11.marks_ref, ...), custom_call_target="tpu_custom_call" | custom-call | tf_op jit(solution)/shard_map/head/pallas_call | solution.py:333
